TPU v7x, 128 devices: a whole 4x4x4 slice. The times are simulated.
128 devices in a mesh: dp: 4 (over z), row: 8 (over x_lo, y), col: 4 (over x_hi, core).
Axes of the slice: x: 4 (x_hi: 2, x_lo: 2; x = x_hi * 2 + x_lo), y: 4, z: 4, core: 2. Of those that a mesh axis runs over, the one named last changes fastest.
Arguments:
- tokens: bfloat16 [32768, 6144], P(('dp', 'row', 'col')), may hold values from -60 to 60
- grads: bfloat16 [32768, 24576], P(('dp', 'row', 'col')), may hold values from -2 to 2
- weight_grad: bfloat16 [6144, 24576], P('row', ('dp', 'col')), may hold values from -0.5 to 0.5
Outputs:
- update: bfloat16 [6144, 24576], P('row', ('dp', 'col'))
All inputs are finite; a program needn't handle non-finite values.
Results may differ from a plain program's by a relative error of at most 0.00065.
The roundings to bfloat16 on the way count: a program that leaves them out, or rounds other values in their place, can miss the bound.
Values may be sent and summed in bfloat16 or wider, within the bound.
No kernel may reach another device: no remote copies, remote signals or barrier semaphores. Data moves between devices by JAX's collectives and lax.ppermute only.
A program may use at most 192 MiB of HBM per device.

v0:
```python
import math
import jax
import jax.numpy as jnp
from jax import lax
from jax.sharding import Mesh
from jax.sharding import PartitionSpec as P

D = 6144
F = 24576
BLOCK = 192
STEPS = 3
ROW = ("row_0", "row_1")
COL = ("col_0", "col_1")
DP_ROW_COL = ("dp", "row_0", "row_1", "col_0", "col_1")
ROW_COL = ("row_0", "row_1", "col_0", "col_1")
DP_COL = ("dp", "col_0", "col_1")
epsilon = 1e-06
damping = 0.01
trust_radius = 0.05


def over_axes(array, axes):
    for axis in axes:
        array = lax.psum(array, axis)
    return array


def newton_inverse(blocks, shift):
    size = blocks.shape[-1]
    identity = jnp.eye(size, dtype=jnp.float32)
    matrix = blocks + shift * identity
    frobenius = jnp.sqrt(jnp.sum(matrix * matrix, axis=(1, 2)))
    iterate = identity[None, :, :] / frobenius[:, None, None]
    for sweep in range(STEPS):
        product = jnp.einsum("nij,njk->nik", matrix, iterate, precision=lax.Precision.HIGHEST)
        iterate = jnp.einsum(
            "nij,njk->nik", iterate, 2.0 * identity - product, precision=lax.Precision.HIGHEST
        )
    return iterate.astype(jnp.bfloat16)


def block_trace(blocks):
    return jnp.sum(jnp.diagonal(blocks, axis1=1, axis2=2))


def on_device(tokens, grads, weight_grad):
    count = tokens.shape[0]
    n_dp = lax.axis_size("dp")
    n_row = lax.axis_size(ROW)
    n_col = lax.axis_size(COL)
    devices_all = n_dp * n_row * n_col
    inverse_count = 1.0 / (count * devices_all)
    blocks_in = D // BLOCK
    blocks_out = F // BLOCK
    per_shard = blocks_out // (n_dp * n_col)
    per_owner = blocks_out // devices_all
    row_blocks = D // n_row // BLOCK
    features = tokens.reshape(count, blocks_in, BLOCK)
    part_in = (
        jnp.einsum("tai,taj->aij", features, features, preferred_element_type=jnp.float32)
        * inverse_count
    )
    received = lax.all_to_all(grads, DP_ROW_COL, split_axis=1, concat_axis=0, tiled=True)
    columns = received.reshape(count * devices_all, per_owner, BLOCK)
    owned_out = (
        jnp.einsum("tai,taj->aij", columns, columns, preferred_element_type=jnp.float32)
        * inverse_count
    )
    summed_in = lax.psum(part_in, DP_ROW_COL)
    owned_in = lax.dynamic_slice_in_dim(summed_in, lax.axis_index(ROW) * row_blocks, row_blocks, 0)
    share_in = block_trace(summed_in) / devices_all
    trace_out, trace_in = (
        over_axes(block_trace(owned_out), DP_ROW_COL),
        over_axes(share_in, DP_ROW_COL),
    )
    ratio = jnp.sqrt((trace_in / D + epsilon) / (trace_out / F + epsilon))
    damp_root = math.sqrt(damping)
    inverse_in = newton_inverse(owned_in, ratio * damp_root)
    inverse_own = newton_inverse(owned_out, damp_root / ratio)
    group_blocks = lax.all_gather(inverse_own, ROW_COL, axis=0, tiled=True)
    inverse_out = lax.dynamic_slice_in_dim(
        group_blocks, lax.axis_index(COL) * per_shard, per_shard, 0
    )
    local_rows, local_cols = weight_grad.shape
    left = jnp.einsum(
        "aij,ajc->aic",
        inverse_in,
        weight_grad.reshape(row_blocks, BLOCK, local_cols),
        preferred_element_type=jnp.float32,
    )
    left = left.reshape(local_rows, local_cols).astype(jnp.bfloat16)
    natural = jnp.einsum(
        "rkj,kji->rki",
        left.reshape(local_rows, per_shard, BLOCK),
        inverse_out,
        preferred_element_type=jnp.float32,
    ).reshape(local_rows, local_cols)
    alignment = over_axes(jnp.sum(natural * weight_grad.astype(jnp.float32)), DP_ROW_COL)
    return (natural * jnp.sqrt(trust_radius * D * F / alignment)).astype(jnp.bfloat16)


def solution(mesh):
    finer = Mesh(
        mesh.devices.reshape(mesh.shape["dp"], 2, 4, 2, 2),
        ("dp", "row_0", "row_1", "col_0", "col_1"),
    )
    placed = (P(DP_ROW_COL, None), P(DP_ROW_COL, None), P(ROW, DP_COL))
    return jax.shard_map(
        on_device, mesh=finer, in_specs=placed, out_specs=P(ROW, DP_COL), check_vma=False
    )
```

profile of v0, /device:TPU:1, one launch (start us, length us, event | category | flops | bytes accessed | tf_op | source)
XLA Modules:
  0.0 519.1 jit_solution(1380360303799974185)
XLA Ops:
  6.5 16.6 %copy.12 = bf16[256,24576]{0,1:T(8,128)(2,1)} copy(bf16[256,24576]{1,0:T(8,128)(2,1)} %param.4) | data formatting | bytes 25165824 | tf_op args[1]
  23.2 11.9 %all-to-all-start = ((bf16[256,128,192]{0,2,1:T(8,128)(2,1)}), bf16[256,128,192]{0,2,1:T(8,128)(2,1)}, u32[]{:S(2)}, u32[]{:S(2)}) async-start(bf16[256,128,192]{0,2,1:T(8,128)(2,1)} %bitcast.37), calls=%async_computation | async-start | bytes 25165824 | tf_op jit(solution)/shard_map/all_to_all | solution.py:63
  35.1 0.0 all-reduce.7.cloned.1.call-start
  35.1 3.2 copy.13
  38.3 3.7 broadcast_multiply_fusion
  42.0 0.0 all-reduce.7.cloned.1.call-update
  42.0 0.0 all-gather.3.cloned.1.call-start
  42.1 284.1 %all-reduce.7.cloned.1.call-done = f32[32,192,192]{2,1,0:T(8,128)} async-done(((f32[32,192,192]{2,1,0:T(8,128)}), f32[32,192,192]{2,1,0:T(8,128)}) %all-reduce.7.cloned.1.call-update) | async-done | bytes 4718608 | tf_op jit(solution)/shard_map/psum | solution.py:69
  326.2 12.2 %copy.14 = f32[32,192,192]{0,2,1:T(8,128)} copy(f32[32,192,192]{2,1,0:T(8,128)} %all-reduce.7.cloned.1.call-done) | data formatting | bytes 9437184 | tf_op jit(solution)/shard_map/psum | solution.py:69
  338.4 4.6 gather_fusion
  343.0 0.6 reduce_sum.45
  344.3 0.0 all-to-all-done
  344.3 11.6 %fusion.7 = f32[192,192]{1,0:T(8,128)S(1)} fusion(bf16[256,128,192]{0,2,1:T(8,128)(2,1)} %all-to-all-done), kind=kOutput, calls=%fused_computation.18 | convolution fusion | flops 2415955968 | bytes 12730368 | tf_op jit(solution)/shard_map/tai,taj->aij/dot_general | solution.py:66
  355.9 1.9 gather_fusion.1
  357.8 0.6 reduce.2
  358.4 9.0 %all-reduce.1 = (f32[]{:T(128)}, f32[]{:T(128)}) all-reduce(f32[]{:T(128)S(6)} %div.43, f32[]{:T(128)} %reduce.2), channel_id=1, replica_groups=mesh['dp'=4,'row_0'=2,'row_1'=4,'col_0'=2,'col_1'=2] {'dp'}, use_global_device_ids=true, to_apply=%region_2.3 | all-reduce | flops 2 | bytes 16 | tf_op jit(solution)/shard_map/psum | solution.py:24
  367.4 4.5 all-reduce.4
  371.9 7.8 %all-reduce = (f32[]{:T(128)}, f32[]{:T(128)}) all-reduce(f32[]{:T(128)} %get-tuple-element.13, f32[]{:T(128)} %get-tuple-element.14), channel_id=1, replica_groups=mesh['dp'=4,'row_0'=2,'row_1'=4,'col_0'=2,'col_1'=2] {'row_1'}, use_global_device_ids=true, to_apply=%region_4.5 | all-reduce | flops 2 | bytes 16 | tf_op jit(solution)/shard_map/psum | solution.py:24
  379.7 6.0 %all-reduce.3 = (f32[]{:T(128)}, f32[]{:T(128)}) all-reduce(f32[]{:T(128)} %get-tuple-element.5, f32[]{:T(128)} %get-tuple-element.6), channel_id=1, replica_groups=mesh['dp'=4,'row_0'=2,'row_1'=4,'col_0'=2,'col_1'=2] {'col_0'}, use_global_device_ids=true, to_apply=%region_5.6 | all-reduce | flops 2 | bytes 16 | tf_op jit(solution)/shard_map/psum | solution.py:24
  385.7 10.4 %all-reduce.2 = (f32[]{:T(128)}, f32[]{:T(128)}) all-reduce(f32[]{:T(128)} %get-tuple-element.11, f32[]{:T(128)} %get-tuple-element.12), channel_id=1, replica_groups=mesh['dp'=4,'row_0'=2,'row_1'=4,'col_0'=2,'col_1'=2] {'col_1'}, use_global_device_ids=true, to_apply=%region_6.7 | all-reduce | flops 2 | bytes 16 | tf_op jit(solution)/shard_map/psum | solution.py:24
  397.4 0.7 multiply_reduce_fusion.2
  398.7 0.3 convolution_subtract_fusion.5
  399.1 0.3 fusion.21
  399.4 0.3 convolution_subtract_fusion.4
  399.7 0.3 fusion.39
  400.1 0.3 convolution_subtract_fusion.3
  400.4 0.9 convolution_convert_fusion.2
  401.4 0.0 all-gather.3.cloned.1.call-update
  401.5 1.3 multiply_reduce_fusion.1
  402.8 2.1 convolution_subtract_fusion.2
  405.0 0.9 fusion.11
  405.9 0.0 copy-start
  405.9 2.2 convolution_subtract_fusion.1
  408.1 0.9 fusion.40
  409.1 2.1 convolution_subtract_fusion
  411.1 0.9 convolution_convert_fusion.1
  412.0 0.0 copy-done
  412.0 2.2 convolution_convert_fusion
  414.2 4.7 convert_element_type.38
  419.0 35.9 %all-gather.3.cloned.1.call-done = bf16[6144,192]{1,0:T(8,128)(2,1)} async-done(((bf16[192,192]{1,0:T(8,128)(2,1)}), bf16[6144,192]{1,0:T(8,128)(2,1)}) %all-gather.3.cloned.1.call-update) | async-done | bytes 2359312 | tf_op jit(solution)/shard_map/all_gather | solution.py:80
  454.9 4.8 fusion.2
  459.7 0.0 copy-start.1
  459.7 6.3 %copy.18 = f32[768,1536]{1,0:T(8,128)} copy(f32[768,1536]{0,1:T(8,128)} %bitcast.41) | data formatting | bytes 9437184 | tf_op jit(solution)/shard_map/reshape | solution.py:97
  466.0 0.0 copy-done.1
  466.0 4.2 multiply_reduce_fusion
  470.1 9.3 %psum.123 = f32[]{:T(128)} all-reduce(f32[]{:T(128)} %multiply_reduce_fusion), channel_id=1, replica_groups=mesh['dp'=4,'row_0'=2,'row_1'=4,'col_0'=2,'col_1'=2] {'dp'}, use_global_device_ids=true, to_apply=%region_16.17 | all-reduce | flops 1 | bytes 8 | tf_op jit(solution)/shard_map/psum | solution.py:24
  479.4 4.4 psum.124
  483.8 8.1 %psum.125 = f32[]{:T(128)} all-reduce(f32[]{:T(128)} %psum.124), channel_id=1, replica_groups=mesh['dp'=4,'row_0'=2,'row_1'=4,'col_0'=2,'col_1'=2] {'row_1'}, use_global_device_ids=true, to_apply=%region_18.19 | all-reduce | flops 1 | bytes 8 | tf_op jit(solution)/shard_map/psum | solution.py:24
  491.9 5.9 %psum.126 = f32[]{:T(128)} all-reduce(f32[]{:T(128)} %psum.125), channel_id=1, replica_groups=mesh['dp'=4,'row_0'=2,'row_1'=4,'col_0'=2,'col_1'=2] {'col_0'}, use_global_device_ids=true, to_apply=%region_19.20 | all-reduce | flops 1 | bytes 8 | tf_op jit(solution)/shard_map/psum | solution.py:24
  497.8 9.4 %psum.127 = f32[]{:T(128)} all-reduce(f32[]{:T(128)} %psum.126), channel_id=1, replica_groups=mesh['dp'=4,'row_0'=2,'row_1'=4,'col_0'=2,'col_1'=2] {'col_1'}, use_global_device_ids=true, to_apply=%region_20.21 | all-reduce | flops 1 | bytes 8 | tf_op jit(solution)/shard_map/psum | solution.py:24
  507.9 4.3 multiply_convert_fusion
  (5 shorter events, 0.1 us)
Async XLA Ops:
  23.2 321.1 %all-to-all-start = ((bf16[256,128,192]{0,2,1:T(8,128)(2,1)}), bf16[256,128,192]{0,2,1:T(8,128)(2,1)}, u32[]{:S(2)}, u32[]{:S(2)}) async-start(bf16[256,128,192]{0,2,1:T(8,128)(2,1)} %bitcast.37), calls=%async_computation | async-start | bytes 25165824 | tf_op jit(solution)/shard_map/all_to_all | solution.py:63
  35.1 291.1 %all-reduce.7.cloned.1.call-start = ((), (), s32[]{:S(2)}) async-start(), calls=%async_computation.1 | async-start | bytes 12582912 | tf_op jit(solution)/shard_map/psum | solution.py:69
  42.0 412.9 %all-gather.3.cloned.1.call-start = ((), (), s32[]{:S(2)}) async-start(), calls=%async_computation.2 | async-start | bytes 3244032 | tf_op jit(solution)/shard_map/all_gather | solution.py:80
  405.9 6.1 %copy-start = (bf16[768,1536]{1,0:T(8,128)(2,1)S(1)}, bf16[768,1536]{1,0:T(8,128)(2,1)}, u32[]{:S(2)}) copy-start(bf16[768,1536]{1,0:T(8,128)(2,1)} %param.5) | copy-start | bytes 7077892
  459.7 6.3 %copy-start.1 = (bf16[768,1536]{1,0:T(8,128)(2,1)S(1)}, bf16[768,1536]{1,0:T(8,128)(2,1)}, u32[]{:S(2)}) copy-start(bf16[768,1536]{1,0:T(8,128)(2,1)} %param.5) | copy-start | bytes 7077892
Sparse Core Ops, SparseCore 0:
  42.1 284.0 all-reduce.6
  401.5 53.3 all-gather.2
where the time goes:
time: 521 us; the launch traced here: 519 us
  waiting for transfers between devices  320 us (61%)
  blocking collectives  74.7 us (14%)
  local copies, waits for them, and re-layouts  49.6 us (10%)
  matrix products  34 us (7%)
  between operations  17 us (3%)
  starting transfers between devices  12 us (2%)
  other arithmetic  11.7 us (2%)
    psum x1, waiting for transfers between devices, on_device(): summed_in = lax.psum(part_in, DP_ROW_COL)  284 us
    psum x10, blocking collectives, over_axes(): array = lax.psum(array, axis)  74.7 us
    all_gather x1, waiting for transfers between devices, on_device(): group_blocks = lax.all_gather(inverse_own, ROW_COL, axis=0, tiled=True)  35.9 us
    unnamed x6, local copies, waits for them, and re-layouts  19.8 us
    psum x1, local copies, waits for them, and re-layouts, on_device(): summed_in = lax.psum(part_in, DP_ROW_COL)  12.2 us
    all_to_all x1, starting transfers between devices, on_device(): lax.all_to_all(grads, DP_ROW_COL, split_axis=1, concat_axis=0, tiled=True)  11.9 us
    dot_general x1, matrix products, on_device(): jnp.einsum('tai,taj->aij', columns, columns, preferred_element_type=jnp.f...  11.6 us
  transfers between devices with their start and end apart: 3, of which 2 were waited for; matrix products, arithmetic and copies ran while one was open for 8% of the time, Pallas kernels for 0%

commit v1 on v0

--- a/solution.py
+++ b/solution.py
@@ -21,7 +21,7 @@
 
 def over_axes(array, axes):
     for axis in axes:
-        array = lax.psum(array, axis)
+        array = jnp.sum(lax.all_gather(array, axis), axis=0)
     return array
 
 

time: 521 us -> 548 us (1.052)
  local copies, waits for them, and re-layouts: 49.6 us -> 73.8 us
  other arithmetic: 11.7 us -> 21.1 us
  blocking collectives: 74.7 us -> 68.1 us
    psum x10 -> x0, blocking collectives: 74.7 us -> none  [over_axes(): array = lax.psum(array, axis)]
    unnamed x0 -> x10, blocking collectives: none -> 68.1 us
    unnamed x6 -> x51, local copies, waits for them, and re-layouts: 19.8 us -> 44.1 us
    reduce_sum x0 -> x15, other arithmetic: none -> 9.35 us  [over_axes(): array = jnp.sum(lax.all_gather(array, axis), axis=0)]
where the time goes in v1:
time: 548 us; the launch traced here: 546 us
  waiting for transfers between devices  320 us (58%)
  local copies, waits for them, and re-layouts  73.8 us (13%)
  blocking collectives  68.1 us (12%)
  matrix products  34.1 us (6%)
  other arithmetic  21.1 us (4%)
  between operations  17.2 us (3%)
  starting transfers between devices  12 us (2%)
    psum x1, waiting for transfers between devices, on_device(): summed_in = lax.psum(part_in, DP_ROW_COL)  284 us
    unnamed x10, blocking collectives  68.1 us
    unnamed x51, local copies, waits for them, and re-layouts  44.1 us
    all_gather x1, waiting for transfers between devices, on_device(): group_blocks = lax.all_gather(inverse_own, ROW_COL, axis=0, tiled=True)  36 us
    psum x1, local copies, waits for them, and re-layouts, on_device(): summed_in = lax.psum(part_in, DP_ROW_COL)  12.2 us
    all_to_all x1, starting transfers between devices, on_device(): lax.all_to_all(grads, DP_ROW_COL, split_axis=1, concat_axis=0, tiled=True)  11.9 us
    dot_general x1, matrix products, on_device(): jnp.einsum('tai,taj->aij', columns, columns, preferred_element_type=jnp.f...  11.6 us
  transfers between devices with their start and end apart: 3, of which 2 were waited for; matrix products, arithmetic and copies ran while one was open for 8% of the time, Pallas kernels for 0%

profile of v1, /device:TPU:1, one launch (start us, length us, event | category | flops | bytes accessed | tf_op | source)
XLA Modules:
  0.0 545.9 jit_solution(639691920309871633)
XLA Ops:
  6.5 16.6 %copy.12 = bf16[256,24576]{0,1:T(8,128)(2,1)} copy(bf16[256,24576]{1,0:T(8,128)(2,1)} %param.4) | data formatting | bytes 25165824 | tf_op args[1]
  23.2 11.9 %all-to-all-start = ((bf16[256,128,192]{0,2,1:T(8,128)(2,1)}), bf16[256,128,192]{0,2,1:T(8,128)(2,1)}, u32[]{:S(2)}, u32[]{:S(2)}) async-start(bf16[256,128,192]{0,2,1:T(8,128)(2,1)} %bitcast.57), calls=%async_computation | async-start | bytes 25165824 | tf_op jit(solution)/shard_map/all_to_all | solution.py:63
  35.1 3.2 copy.13
  38.3 3.7 broadcast_multiply_fusion
  42.6 0.6 dynamic-slice
  43.2 283.7 %all-reduce.22.cloned.1.call-done = f32[32,192,192]{2,1,0:T(8,128)} async-done(((f32[32,192,192]{2,1,0:T(8,128)}), f32[32,192,192]{2,1,0:T(8,128)}) %all-reduce.22.cloned.1.call-update) | async-done | bytes 4718608 | tf_op jit(solution)/shard_map/psum | solution.py:69
  327.0 12.2 %copy.14 = f32[32,192,192]{0,2,1:T(8,128)} copy(f32[32,192,192]{2,1,0:T(8,128)} %all-reduce.22.cloned.1.call-done) | data formatting | bytes 9437184 | tf_op jit(solution)/shard_map/psum | solution.py:69
  339.2 4.6 gather_fusion
  343.8 0.6 reduce_sum.180
  345.1 0.7 dynamic-update-slice
  345.8 11.6 %fusion.7 = f32[192,192]{1,0:T(8,128)S(1)} fusion(bf16[256,128,192]{0,2,1:T(8,128)(2,1)} %all-to-all-done), kind=kOutput, calls=%fused_computation.18 | convolution fusion | flops 2415955968 | bytes 12730368 | tf_op jit(solution)/shard_map/tai,taj->aij/dot_general | solution.py:66
  357.4 1.9 gather_fusion.1
  359.9 1.4 dynamic-update-slice.5
  361.3 0.6 dynamic-slice.1
  361.9 8.4 %all-reduce.16 = (f32[4]{0:T(128)S(1)}, f32[4]{0:T(128)S(1)}) all-reduce(f32[4]{0:T(128)S(1)} %dynamic-update-slice, f32[4]{0:T(128)S(1)} %dynamic-update-slice.5), channel_id=1, replica_groups=mesh['dp'=4,'row_0'=2,'row_1'=4,'col_0'=2,'col_1'=2] {'dp'}, use_global_device_ids=true, to_apply=%add | all-reduce | flops 8 | bytes 64
  370.3 0.6 reduce_sum.181
  370.9 0.7 reduce_sum.187
  371.6 1.4 dynamic-update-slice.1
  373.0 1.4 dynamic-update-slice.6
  374.4 0.7 dynamic-slice.2
  375.1 3.8 all-reduce.19
  378.8 0.7 reduce_sum.188
  380.1 1.5 dynamic-update-slice.7
  381.6 1.4 dynamic-update-slice.2
  383.0 0.7 dynamic-slice.3
  383.7 7.2 %all-reduce.15 = (f32[4]{0:T(128)S(1)}, f32[4]{0:T(128)S(1)}) all-reduce(f32[4]{0:T(128)S(1)} %dynamic-update-slice.2, f32[4]{0:T(128)S(1)} %dynamic-update-slice.7), channel_id=1, replica_groups=mesh['dp'=4,'row_0'=2,'row_1'=4,'col_0'=2,'col_1'=2] {'row_1'}, use_global_device_ids=true, to_apply=%add.2 | all-reduce | flops 8 | bytes 64
  390.9 0.7 reduce_sum.189
  392.1 1.4 dynamic-update-slice.8
  393.6 1.4 dynamic-update-slice.3
  395.0 0.7 dynamic-slice.4
  395.6 5.3 all-reduce.18
  400.9 0.7 reduce_sum.190
  402.2 1.5 dynamic-update-slice.9
  403.6 1.4 dynamic-update-slice.4
  405.1 9.7 %all-reduce.17 = (f32[2]{0:T(128)S(1)}, f32[2]{0:T(128)S(1)}) all-reduce(f32[2]{0:T(128)S(1)} %dynamic-update-slice.4, f32[2]{0:T(128)S(1)} %dynamic-update-slice.9), channel_id=1, replica_groups=mesh['dp'=4,'row_0'=2,'row_1'=4,'col_0'=2,'col_1'=2] {'col_1'}, use_global_device_ids=true, to_apply=%add.4 | all-reduce | flops 4 | bytes 32
  417.4 0.7 multiply_reduce_fusion.2
  420.4 1.0 convolution_convert_fusion.2
  421.5 1.3 multiply_reduce_fusion.1
  422.8 2.1 convolution_subtract_fusion.2
  425.0 0.9 fusion.11
  426.0 2.2 convolution_subtract_fusion.1
  428.2 0.9 fusion.40
  429.1 2.1 convolution_subtract_fusion
  431.2 0.9 convolution_convert_fusion.1
  432.1 2.2 convolution_convert_fusion
  434.3 4.7 convert_element_type.38
  439.0 36.0 %all-gather.3.cloned.1.call-done = bf16[6144,192]{1,0:T(8,128)(2,1)} async-done(((bf16[192,192]{1,0:T(8,128)(2,1)}), bf16[6144,192]{1,0:T(8,128)(2,1)}) %all-gather.3.cloned.1.call-update) | async-done | bytes 2359312 | tf_op jit(solution)/shard_map/all_gather | solution.py:80
  475.0 4.9 fusion.2
  479.9 6.2 %copy.18 = f32[768,1536]{1,0:T(8,128)} copy(f32[768,1536]{0,1:T(8,128)} %bitcast.61) | data formatting | bytes 9437184 | tf_op jit(solution)/shard_map/reshape | solution.py:97
  486.0 4.2 multiply_reduce_fusion
  490.2 1.4 dynamic-update-slice.10
  491.6 8.8 %all-reduce.10 = f32[4]{0:T(128)S(1)} all-reduce(f32[4]{0:T(128)S(1)} %dynamic-update-slice.10), channel_id=1, replica_groups=mesh['dp'=4,'row_0'=2,'row_1'=4,'col_0'=2,'col_1'=2] {'dp'}, use_global_device_ids=true, to_apply=%add.10 | all-reduce | flops 4 | bytes 32
  500.3 0.6 reduce_sum.195
  500.9 1.4 dynamic-update-slice.11
  502.3 3.8 all-reduce.11
  506.1 0.6 reduce_sum.196
  506.7 1.4 dynamic-update-slice.12
  508.1 7.3 %all-reduce.12 = f32[4]{0:T(128)S(1)} all-reduce(f32[4]{0:T(128)S(1)} %dynamic-update-slice.12), channel_id=1, replica_groups=mesh['dp'=4,'row_0'=2,'row_1'=4,'col_0'=2,'col_1'=2] {'row_1'}, use_global_device_ids=true, to_apply=%add.12 | all-reduce | flops 4 | bytes 32
  515.4 0.6 reduce_sum.197
  516.0 1.4 dynamic-update-slice.13
  517.4 5.3 all-reduce.13
  523.3 1.4 dynamic-update-slice.14
  524.7 8.7 %all-reduce.14 = f32[2]{0:T(128)S(1)} all-reduce(f32[2]{0:T(128)S(1)} %dynamic-update-slice.14), channel_id=1, replica_groups=mesh['dp'=4,'row_0'=2,'row_1'=4,'col_0'=2,'col_1'=2] {'col_1'}, use_global_device_ids=true, to_apply=%add.14 | all-reduce | flops 2 | bytes 16
  534.8 4.3 multiply_convert_fusion
  (52 shorter events, 7.2 us)
Async XLA Ops:
  23.2 322.6 %all-to-all-start = ((bf16[256,128,192]{0,2,1:T(8,128)(2,1)}), bf16[256,128,192]{0,2,1:T(8,128)(2,1)}, u32[]{:S(2)}, u32[]{:S(2)}) async-start(bf16[256,128,192]{0,2,1:T(8,128)(2,1)} %bitcast.57), calls=%async_computation | async-start | bytes 25165824 | tf_op jit(solution)/shard_map/all_to_all | solution.py:63
  35.1 291.9 %all-reduce.22.cloned.1.call-start = ((), (), s32[]{:S(2)}) async-start(), calls=%async_computation.1 | async-start | bytes 12582912 | tf_op jit(solution)/shard_map/psum | solution.py:69
  42.0 0.7 copy-start.6
  42.0 433.0 %all-gather.3.cloned.1.call-start = ((), (), s32[]{:S(2)}) async-start(), calls=%async_computation.2 | async-start | bytes 3244032 | tf_op jit(solution)/shard_map/all_gather | solution.py:80
  345.8 15.5 %copy-start.5 = (u32[128]{0:T(128)S(1)}, u32[128]{0:T(128)}, u32[]{:S(2)}) copy-start(u32[128]{0:T(128)} %constant.98) | copy-start | bytes 1540
  345.8 28.7 %copy-start.4 = (u32[128]{0:T(128)S(1)}, u32[128]{0:T(128)}, u32[]{:S(2)}) copy-start(u32[128]{0:T(128)} %constant.103) | copy-start | bytes 1540
  345.8 37.3 %copy-start.3 = (u32[128]{0:T(128)S(1)}, u32[128]{0:T(128)}, u32[]{:S(2)}) copy-start(u32[128]{0:T(128)} %constant.108) | copy-start | bytes 1540
  345.8 49.2 %copy-start.2 = (u32[128]{0:T(128)S(1)}, u32[128]{0:T(128)}, u32[]{:S(2)}) copy-start(u32[128]{0:T(128)} %constant.113) | copy-start | bytes 1540
  425.9 6.1 %copy-start = (bf16[768,1536]{1,0:T(8,128)(2,1)S(1)}, bf16[768,1536]{1,0:T(8,128)(2,1)}, u32[]{:S(2)}) copy-start(bf16[768,1536]{1,0:T(8,128)(2,1)} %param.5) | copy-start | bytes 7077892
  479.8 6.2 %copy-start.1 = (bf16[768,1536]{1,0:T(8,128)(2,1)S(1)}, bf16[768,1536]{1,0:T(8,128)(2,1)}, u32[]{:S(2)}) copy-start(bf16[768,1536]{1,0:T(8,128)(2,1)} %param.5) | copy-start | bytes 7077892
Sparse Core Ops, SparseCore 0:
  42.1 284.7 all-reduce.21
  421.5 53.4 all-gather.2
